TPU v7x, 32 devices: a whole 2x2x4 slice. The times are simulated.
32 devices in a mesh: chain: 8 (over y, x, core), col: 4 (over z).
Axes of the slice: x: 2, y: 2, z: 4, core: 2. Of those that a mesh axis runs over, the one named last changes fastest.
Arguments:
- rhs: bfloat16 [16, 64, 2560], P('chain', None, 'col'), may hold values from -6 to 6
- block_inverse: bfloat16 [16, 2560, 2560], P('chain', 'col'), as said below
- entry_factor: bfloat16 [16, 2560, 128], P('chain', 'col'), as said below
- exit_factor: bfloat16 [16, 2560, 128], P('chain', 'col'), as said below
- previous: bfloat16 [64, 2560], P(None, 'col'), may hold values from -6 to 6
Outputs:
- solution: float32 [16, 64, 2560], P('chain', None, 'col')
Inputs may be any that keep to these rules, and one draw needn't show every extreme that they name: Every block of block_inverse equals its own transpose. `entry_factor`: entries are independent, of mean zero. `exit_factor`: entries are independent, of mean zero.
All inputs are finite; a program needn't handle non-finite values.
Results may differ from a plain program's by a relative error of at most 0.0003.
Values may be sent and summed in bfloat16 or wider, within the bound.
A program may use at most 64 MiB of HBM per device.

v0:
```python
import jax
import jax.numpy as jnp
from jax import lax
from jax.sharding import PartitionSpec as P


def from_behind(block, axis, distance):
    devices = range(lax.axis_size(axis))
    route = [(i - distance, i) for i in devices if i - distance in devices]
    return lax.ppermute(block, axis, route)


def entering(part, axis, combine, identity, reverse):
    count = lax.axis_size(axis)
    place = lax.axis_index(axis)
    ahead = count - 1 - place if reverse else place
    gathered = jax.tree.map(lambda a: lax.all_gather(a, axis), part)
    state = jax.tree.map(lambda a, e: jnp.zeros_like(a) + jnp.asarray(e, a.dtype), part, identity)

    def one(step, state):
        source = count - 1 - step if reverse else step
        return combine(
            state, jax.tree.map(lambda a: lax.dynamic_index_in_dim(a, source, 0, False), gathered)
        )

    return lax.fori_loop(0, ahead, one, state)


def compose(earlier, later):
    exact = lax.Precision.HIGHEST
    first_map, first_shift = earlier
    second_map, second_shift = later
    return (
        jnp.dot(first_map, second_map, precision=exact),
        jnp.dot(first_shift, second_map, precision=exact) + second_shift,
    )


def shards(rhs, block_inverse, entry_factor, exit_factor, previous):
    exact = lax.Precision.HIGHEST
    intervals_here = rhs.shape[0]
    column_count = rhs.shape[1]
    state_width = entry_factor.shape[2]
    arriving = from_behind(exit_factor[:1], "chain", -1)
    following = jnp.concatenate([exit_factor[1:], arriving], axis=0)
    couple_part = -jnp.einsum(
        "irn,irm->inm", entry_factor, following, preferred_element_type=jnp.float32
    )
    source_part = jnp.einsum("icr,irm->icm", rhs, following, preferred_element_type=jnp.float32)
    opening_part = jnp.dot(previous, exit_factor[0], preferred_element_type=jnp.float32)
    couple, source, opening = lax.psum((couple_part, source_part, opening_part), "col")
    identity = jnp.eye(state_width, dtype=jnp.float32)
    empty_shift = jnp.zeros((column_count, state_width), jnp.float32)
    first_chain = lax.axis_index("chain") == 0
    matrix = identity
    offset = empty_shift
    for position in range(intervals_here):
        matrix = jnp.dot(matrix, couple[position], precision=exact)
        offset = jnp.dot(offset, couple[position], precision=exact) + source[position]
    folded = jnp.dot(opening, matrix, precision=exact) + offset
    offset = jnp.where(first_chain, folded, offset)
    matrix = jnp.where(first_chain, jnp.zeros_like(matrix), matrix)
    _, incoming = entering((matrix, offset), "chain", compose, (identity, empty_shift), False)
    carry_state = jnp.where(first_chain, opening, incoming)
    solved_list = []
    for position in range(intervals_here):
        solved_list.append(
            rhs[position].astype(jnp.float32)
            - jnp.dot(carry_state, entry_factor[position].astype(jnp.float32).T, precision=exact)
        )
        carry_state = jnp.dot(carry_state, couple[position], precision=exact) + source[position]
    forward = jnp.stack(solved_list).astype(jnp.bfloat16)
    applied = jnp.einsum(
        "icb,irb->icr",
        lax.all_gather(forward, "col", axis=2, tiled=True),
        block_inverse,
        preferred_element_type=jnp.float32,
    )
    carried_part = jnp.einsum(
        "icr,irn->icn",
        applied.astype(jnp.bfloat16),
        entry_factor,
        preferred_element_type=jnp.float32,
    )
    carried = lax.psum(carried_part, "col")
    last_chain = lax.axis_index("chain") == lax.axis_size("chain") - 1
    matrix = identity
    offset = empty_shift
    for position in reversed(range(intervals_here)):
        turned = couple[position].T
        matrix = jnp.dot(matrix, turned, precision=exact)
        offset = jnp.dot(offset, turned, precision=exact) + carried[position]
    matrix = jnp.where(last_chain, jnp.zeros_like(matrix), matrix)
    _, behind = entering((matrix, offset), "chain", compose, (identity, empty_shift), True)
    results = [None] * intervals_here
    for position in reversed(range(intervals_here)):
        results[position] = applied[position] - jnp.dot(
            behind, following[position].astype(jnp.float32).T, precision=exact
        )
        behind = jnp.dot(behind, couple[position].T, precision=exact) + carried[position]
    return jnp.stack(results)


def solution(mesh):
    placed = (
        P("chain", None, "col"),
        P("chain", "col", None),
        P("chain", "col", None),
        P("chain", "col", None),
        P(None, "col"),
    )
    return jax.shard_map(
        shards, mesh=mesh, in_specs=placed, out_specs=P("chain", None, "col"), check_vma=False
    )
```

profile of v0, /device:TPU:0, one launch (start us, length us, event | category | flops | bytes accessed | tf_op | source)
XLA Modules:
  0.0 161.5 jit_solution(1179635024437629665)
XLA Ops:
  6.5 1.1 fusion.37
  7.8 1.3 collective-permute-start
  9.3 1.8 %collective-permute-done = bf16[1,640,128]{1,2,0:T(8,128)(2,1)S(1)} collective-permute-done((bf16[1,640,128]{1,2,0:T(8,128)(2,1)S(1)}, bf16[1,640,128]{1,2,0:T(8,128)(2,1)S(1)}, u32[]{:S(2)}, u32[]{:S(2)}) %collective-permute-start) | collective-permute-done | bytes 163872 | tf_op jit(solution)/shard_map/ppermute | solution.py:10
  11.1 1.8 %convolution_bitcast_fusion.2 = f32[2,64,128]{2,1,0:T(8,128)} fusion(bf16[2,64,640]{2,1,0:T(8,128)(2,1)} %param.9, bf16[1,640,128]{1,2,0:T(8,128)(2,1)S(1)} %collective-permute-done, bf16[1,640,128]{1,2,0:T(8,128)(2,1)S(1)} %copy.11), kind=kOutput, calls=%fused_computation.23 | convolution fusion | flops 21135360 | bytes 557056 | tf_op jit(solution)/shard_map/icr,irm->icm/dot_general | solution.py:49
  12.9 1.9 %fusion.10 = f32[2,128,128]{1,2,0:T(8,128)} fusion(bf16[2,640,128]{2,1,0:T(8,128)(2,1)} %param.11, bf16[1,640,128]{1,2,0:T(8,128)(2,1)S(1)} %collective-permute-done, bf16[1,640,128]{1,2,0:T(8,128)(2,1)S(1)} %copy.11), kind=kOutput, calls=%fused_computation.17 | convolution fusion | flops 42139648 | bytes 786432 | tf_op jit(solution)/shard_map/irn,irm->inm/dot_general | solution.py:46
  14.8 1.1 fusion.17
  15.9 21.0 %psum.28 = f32[64,128]{1,0:T(8,128)S(1)} all-reduce(f32[64,128]{1,0:T(8,128)S(1)} %fusion.17), channel_id=1, replica_groups=mesh['chain'=8,'col'=4] {'col'}, use_global_device_ids=true, to_apply=%region_0.0 | all-reduce | flops 8192 | bytes 65536 | tf_op jit(solution)/shard_map/psum | solution.py:51
  36.9 18.5 %all-reduce.6.cloned.1.call-done = (f32[2,128,128]{1,2,0:T(8,128)}, f32[2,64,128]{2,1,0:T(8,128)}) async-done(((f32[2,128,128]{1,2,0:T(8,128)}, f32[2,64,128]{2,1,0:T(8,128)}), (f32[2,128,128]{1,2,0:T(8,128)}, f32[2,64,128]{2,1,0:T(8,128)})) %all-reduce.6.cloned.1.call-update) | async-done | bytes 196624 | tf_op jit(solution)/shard_map/psum | solution.py:51
  55.4 1.1 fusion.27
  56.5 1.1 convolution_add_fusion.5
  57.6 1.1 convolution_add_fusion.4
  58.7 1.1 broadcast_select_fusion
  60.0 9.2 %all-gather.1 = f32[512,128]{1,0:T(8,128)S(1)} all-gather(f32[64,128]{1,0:T(8,128)S(1)} %fusion.15), channel_id=3, replica_groups=mesh['chain'=8,'col'=4] {'chain'}, dimensions={0}, use_global_device_ids=true | all-gather | bytes 294912 | tf_op jit(solution)/shard_map/all_gather | solution.py:17
  69.2 9.8 %all-gather = f32[1024,128]{1,0:T(8,128)S(1)} all-gather(f32[128,128]{1,0:T(8,128)S(1)} %get-tuple-element.159), channel_id=2, replica_groups=mesh['chain'=8,'col'=4] {'chain'}, dimensions={0}, use_global_device_ids=true | all-gather | bytes 589824 | tf_op jit(solution)/shard_map/all_gather | solution.py:17
  79.3 1.1 convolution_add_fusion.3
  80.5 1.0 fusion.26
  81.9 17.2 %all_gather.31 = bf16[2,64,2560]{2,1,0:T(8,128)(2,1)S(1)} all-gather(bf16[2,64,640]{2,1,0:T(8,128)(2,1)S(1)} %pad_maximum_fusion.4), channel_id=1, replica_groups=mesh['chain'=8,'col'=4] {'col'}, dimensions={2}, use_global_device_ids=true | all-gather | bytes 819200 | tf_op jit(solution)/shard_map/all_gather | solution.py:75
  99.1 4.9 %fusion.38 = f32[2,64,640]{2,1,0:T(8,128)S(1)} fusion(bf16[2,64,2560]{2,1,0:T(8,128)(2,1)S(1)} %all_gather.31, bf16[2,640,2560]{2,1,0:T(8,128)(2,1)} %param.10), kind=kOutput, calls=%fused_computation.68 | convolution fusion | flops 419430400 | bytes 7536640 | tf_op jit(solution)/shard_map/icb,irb->icr/dot_general | solution.py:73
  105.1 9.9 %all-gather.2 = f32[1024,128]{1,0:T(8,128)S(1)} all-gather(f32[128,128]{1,0:T(8,128)S(1)} %convolution_select_fusion), channel_id=4, replica_groups=mesh['chain'=8,'col'=4] {'chain'}, dimensions={0}, use_global_device_ids=true | all-gather | bytes 589824 | tf_op jit(solution)/shard_map/all_gather | solution.py:17
  115.0 24.6 %all-reduce.4.cloned.1.call-done = f32[2,64,128]{2,1,0:T(8,128)} async-done(((f32[2,64,128]{2,1,0:T(8,128)}), f32[2,64,128]{2,1,0:T(8,128)}) %all-reduce.4.cloned.1.call-update) | async-done | bytes 65552 | tf_op jit(solution)/shard_map/psum | solution.py:85
  140.5 0.9 convolution_add_fusion.1
  141.5 9.3 %all-gather.3 = f32[512,128]{1,0:T(8,128)S(1)} all-gather(f32[64,128]{1,0:T(8,128)S(1)} %convolution_add_fusion.1), channel_id=5, replica_groups=mesh['chain'=8,'col'=4] {'chain'}, dimensions={0}, use_global_device_ids=true | all-gather | bytes 294912 | tf_op jit(solution)/shard_map/all_gather | solution.py:17
  150.8 1.6 %while.27 = (s32[]{:T(128)}, f32[64,128]{1,0:T(8,128)S(1)}, s32[]{:T(128)}, f32[8,128,128]{2,1,0:T(8,128)S(1)}, f32[8,64,128]{2,1,0:T(8,128)S(1)}, /*index=5*/s32[]{:T(128)}, s32[]{:T(128)}, s32[]{:T(128)}, s32[]{:T(128)}) while((s32[]{:T(128)}, f32[64,128]{1,0:T(8,128)S(1)}, s32[]{:T(128)}, f32[8,128,128]{2,1,0:T(8,128)S(1)}, ...), condition=%wide.region_7.8_spmd, body=%wide.region_6.7_spmd.sunk | while | flops 12591110 | bytes 230539 | solution.py:26
  152.4 0.9 convolution_add_fusion
  (43 shorter events, 5.9 us)
Async XLA Ops:
  6.5 8.3 %copy-start = (bf16[64,640]{1,0:T(8,128)(2,1)S(1)}, bf16[64,640]{1,0:T(8,128)(2,1)}, u32[]{:S(2)}) copy-start(bf16[64,640]{1,0:T(8,128)(2,1)} %param.13) | copy-start | bytes 245764
  6.5 72.5 %copy-start.4 = (bf16[2,64,640]{2,1,0:T(8,128)(2,1)S(1)}, bf16[2,64,640]{2,1,0:T(8,128)(2,1)}, u32[]{:S(2)}) copy-start(bf16[2,64,640]{2,1,0:T(8,128)(2,1)} %param.9) | copy-start | bytes 491524
  6.5 72.5 %copy-start.2 = (bf16[2,640,128]{2,1,0:T(8,128)(2,1)S(1)}, bf16[2,640,128]{2,1,0:T(8,128)(2,1)}, u32[]{:S(2)}) copy-start(bf16[2,640,128]{2,1,0:T(8,128)(2,1)} %param.11) | copy-start | bytes 983044
  6.5 48.9 %all-reduce.6.cloned.1.call-start = ((), (), s32[]{:S(2)}) async-start(), calls=%async_computation.1 | async-start | bytes 393216 | tf_op jit(solution)/shard_map/psum | solution.py:51
  7.8 3.3 %collective-permute-start = (bf16[1,640,128]{1,2,0:T(8,128)(2,1)S(1)}, bf16[1,640,128]{1,2,0:T(8,128)(2,1)S(1)}, u32[]{:S(2)}, u32[]{:S(2)}) collective-permute-start(bf16[1,640,128]{1,2,0:T(8,128)(2,1)S(1)} %copy.10), channel_id=1, source_target_pairs={{4,0},{8,4},{12,8},{16,12},{20,16},{24,20},{28,24},{5,1},{9,5},{13... | collective-permute-start | bytes 491528 | tf_op jit(solution)/shard_map/ppermute | solution.py:10
  14.8 124.8 %all-reduce.4.cloned.1.call-start = ((), (), s32[]{:S(2)}) async-start(), calls=%async_computation | async-start | bytes 131072 | tf_op jit(solution)/shard_map/psum | solution.py:85
  59.8 45.1 %copy-start.1 = (f32[2,128,128]{1,2,0:T(8,128)S(1)}, f32[2,128,128]{1,2,0:T(8,128)}, u32[]{:S(2)}) copy-start(f32[2,128,128]{1,2,0:T(8,128)} %get-tuple-element.155) | copy-start | bytes 393220
  79.3 74.0 %copy-start.3 = (bf16[2,640,128]{2,1,0:T(8,128)(2,1)S(1)}, bf16[2,640,128]{2,1,0:T(8,128)(2,1)}, u32[]{:S(2)}) copy-start(bf16[2,640,128]{2,1,0:T(8,128)(2,1)} %param.12) | copy-start | bytes 983044
Sparse Core Ops, SparseCore 0:
  14.9 40.4 all-reduce.5
  105.0 34.5 all-reduce.3
where the time goes:
time: 162 us; the launch traced here: 161 us
  blocking collectives  76.4 us (47%)
  waiting for transfers between devices  45 us (28%)
  matrix products  22.7 us (14%)
  between operations  13.6 us (8%)
    all_gather x4, blocking collectives, entering(): gathered = jax.tree.map(lambda a: lax.all_gather(a, axis), part)  38.2 us
    psum x1, waiting for transfers between devices, shards(): carried = lax.psum(carried_part, 'col')  24.6 us
    psum x1, blocking collectives, shards(): lax.psum((couple_part, source_part, opening_part), 'col')  21 us
    psum x1, waiting for transfers between devices, shards(): lax.psum((couple_part, source_part, opening_part), 'col')  18.5 us
    all_gather x1, blocking collectives, shards(): lax.all_gather(forward, 'col', axis=2, tiled=True)  17.2 us
    dot_general x1, matrix products, shards(): jnp.einsum('icb,irb->icr', lax.all_gather(forward, 'col', axis=2, tiled=T...  4.94 us
  transfers between devices with their start and end apart: 3, of which 3 were waited for; matrix products, arithmetic and copies ran while one was open for 1% of the time, Pallas kernels for 0%

commit v1 on v0

--- a/solution.py
+++ b/solution.py
@@ -70,12 +70,38 @@
         )
         carry_state = jnp.dot(carry_state, couple[position], precision=exact) + source[position]
     forward = jnp.stack(solved_list).astype(jnp.bfloat16)
-    applied = jnp.einsum(
+    size, index, rows = (lax.axis_size("col"), lax.axis_index("col"), forward.shape[2])
+    right = [(i_2, (i_2 + 1) % size) for i_2 in range(size)]
+    left = [(i_2, (i_2 - 1) % size) for i_2 in range(size)]
+    half = size // 2
+    from_left = from_right = forward
+    so_far = jnp.einsum(
         "icb,irb->icr",
-        lax.all_gather(forward, "col", axis=2, tiled=True),
-        block_inverse,
+        forward,
+        lax.dynamic_slice_in_dim(block_inverse, index * rows, forward.shape[2], axis=2),
         preferred_element_type=jnp.float32,
     )
+    for lap in range(1, half + 1):
+        from_left = lax.ppermute(from_left, "col", right)
+        if lap < size - half:
+            from_right = lax.ppermute(from_right, "col", left)
+            so_far = so_far + jnp.einsum(
+                "icb,irb->icr",
+                from_right,
+                lax.dynamic_slice_in_dim(
+                    block_inverse, (index + lap) % size * rows, from_right.shape[2], axis=2
+                ),
+                preferred_element_type=jnp.float32,
+            )
+        so_far = so_far + jnp.einsum(
+            "icb,irb->icr",
+            from_left,
+            lax.dynamic_slice_in_dim(
+                block_inverse, (index - lap) % size * rows, from_left.shape[2], axis=2
+            ),
+            preferred_element_type=jnp.float32,
+        )
+    applied = so_far
     carried_part = jnp.einsum(
         "icr,irn->icn",
         applied.astype(jnp.bfloat16),

time: 162 us -> 156 us (0.963)
  blocking collectives: 76.4 us -> 59.2 us
  matrix products: 22.7 us -> 26.9 us
  starting transfers between devices: 1.34 us -> 5.21 us
  waiting for transfers between devices: 45 us -> 47.8 us
    all_gather x1 -> x0, blocking collectives: 17.2 us -> none  [shards(): lax.all_gather(forward, 'col', axis=2, tiled=True)]
    ppermute x0 -> x3, waiting for transfers between devices: none -> 4.02 us  [the longest x2 3.51 us: shards(): from_left = lax.ppermute(from_left, 'col', right)]
    ppermute x0 -> x3, starting transfers between devices: none -> 3.88 us  [the longest x1 2.27 us: shards(): from_right = lax.ppermute(from_right, 'col', left)]
    dot_general x1 -> x4, matrix products: 4.94 us -> 8.32 us  [the longest x2 4.14 us: shards(): jnp.einsum('icb,irb->icr', from_left, lax.dynamic_slice_in_dim(block_inve...]
  transfers between devices with their start and end apart: 3 -> 6, of which waited for: 3 -> 6; matrix products, arithmetic and copies ran while one was open for 1% -> 6% of each run, Pallas kernels for 0% -> 0%
where the time goes in v1:
time: 156 us; the launch traced here: 155 us
  blocking collectives  59.2 us (38%)
  waiting for transfers between devices  47.8 us (31%)
  matrix products  26.9 us (17%)
  between operations  13.7 us (9%)
  starting transfers between devices  5.21 us (3%)
    all_gather x4, blocking collectives, entering(): gathered = jax.tree.map(lambda a: lax.all_gather(a, axis), part)  38.2 us
    psum x1, waiting for transfers between devices, shards(): carried = lax.psum(carried_part, 'col')  23.5 us
    psum x1, blocking collectives, shards(): lax.psum((couple_part, source_part, opening_part), 'col')  21 us
    psum x1, waiting for transfers between devices, shards(): lax.psum((couple_part, source_part, opening_part), 'col')  18.5 us
    dot_general x2, matrix products, shards(): jnp.einsum('icb,irb->icr', from_left, lax.dynamic_slice_in_dim(block_inve...  4.14 us
    ppermute x2, waiting for transfers between devices, shards(): from_left = lax.ppermute(from_left, 'col', right)  3.51 us
  transfers between devices with their start and end apart: 6, of which 6 were waited for; matrix products, arithmetic and copies ran while one was open for 6% of the time, Pallas kernels for 0%

profile of v1, /device:TPU:0, one launch (start us, length us, event | category | flops | bytes accessed | tf_op | source)
XLA Modules:
  0.0 155.3 jit_solution(13371388299988218290)
XLA Ops:
  6.5 1.1 fusion.66
  7.8 1.3 collective-permute-start
  9.3 1.7 %collective-permute-done = bf16[1,640,128]{1,2,0:T(8,128)(2,1)S(1)} collective-permute-done((bf16[1,640,128]{1,2,0:T(8,128)(2,1)S(1)}, bf16[1,640,128]{1,2,0:T(8,128)(2,1)S(1)}, u32[]{:S(2)}, u32[]{:S(2)}) %collective-permute-start) | collective-permute-done | bytes 163872 | tf_op jit(solution)/shard_map/ppermute | solution.py:10
  11.1 1.8 %convolution_bitcast_fusion.2 = f32[2,64,128]{2,1,0:T(8,128)} fusion(bf16[2,64,640]{2,1,0:T(8,128)(2,1)} %param.9, bf16[1,640,128]{1,2,0:T(8,128)(2,1)S(1)} %collective-permute-done, bf16[1,640,128]{1,2,0:T(8,128)(2,1)S(1)} %copy.11), kind=kOutput, calls=%fused_computation.30 | convolution fusion | flops 21135360 | bytes 557056 | tf_op jit(solution)/shard_map/icr,irm->icm/dot_general | solution.py:49
  12.9 1.9 %fusion.25 = f32[2,128,128]{1,2,0:T(8,128)} fusion(bf16[2,640,128]{2,1,0:T(8,128)(2,1)} %param.11, bf16[1,640,128]{1,2,0:T(8,128)(2,1)S(1)} %collective-permute-done, bf16[1,640,128]{1,2,0:T(8,128)(2,1)S(1)} %copy.11), kind=kOutput, calls=%fused_computation.24 | convolution fusion | flops 42139648 | bytes 786432 | tf_op jit(solution)/shard_map/irn,irm->inm/dot_general | solution.py:46
  15.9 21.0 %psum.28 = f32[64,128]{1,0:T(8,128)S(1)} all-reduce(f32[64,128]{1,0:T(8,128)S(1)} %fusion.39), channel_id=1, replica_groups=mesh['chain'=8,'col'=4] {'col'}, use_global_device_ids=true, to_apply=%region_0.0 | all-reduce | flops 8192 | bytes 65536 | tf_op jit(solution)/shard_map/psum | solution.py:51
  36.9 18.5 %all-reduce.6.cloned.1.call-done = (f32[2,128,128]{1,2,0:T(8,128)}, f32[2,64,128]{2,1,0:T(8,128)}) async-done(((f32[2,128,128]{1,2,0:T(8,128)}, f32[2,64,128]{2,1,0:T(8,128)}), (f32[2,128,128]{1,2,0:T(8,128)}, f32[2,64,128]{2,1,0:T(8,128)})) %all-reduce.6.cloned.1.call-update) | async-done | bytes 196624 | tf_op jit(solution)/shard_map/psum | solution.py:51
  56.5 1.1 convolution_add_fusion.5
  57.6 1.1 convolution_add_fusion.4
  58.7 1.1 broadcast_select_fusion
  60.0 9.2 %all-gather.1 = f32[512,128]{1,0:T(8,128)S(1)} all-gather(f32[64,128]{1,0:T(8,128)S(1)} %fusion.30), channel_id=3, replica_groups=mesh['chain'=8,'col'=4] {'chain'}, dimensions={0}, use_global_device_ids=true | all-gather | bytes 294912 | tf_op jit(solution)/shard_map/all_gather | solution.py:17
  69.2 9.8 %all-gather = f32[1024,128]{1,0:T(8,128)S(1)} all-gather(f32[128,128]{1,0:T(8,128)S(1)} %get-tuple-element.159), channel_id=2, replica_groups=mesh['chain'=8,'col'=4] {'chain'}, dimensions={0}, use_global_device_ids=true | all-gather | bytes 589824 | tf_op jit(solution)/shard_map/all_gather | solution.py:17
  79.3 1.1 convolution_add_fusion.3
  80.8 1.6 %collective-permute-start.2 = (bf16[2,64,640]{2,1,0:T(8,128)(2,1)S(1)}, bf16[2,64,640]{2,1,0:T(8,128)(2,1)S(1)}, u32[]{:S(2)}, u32[]{:S(2)}) collective-permute-start(bf16[2,64,640]{2,1,0:T(8,128)(2,1)S(1)} %pad_maximum_fusion.4), channel_id=1, source_target_pairs={{0,1},{1,2},{2,3},{3,0},{4,5},{5,6},{6,7},{7,4},{8,9},{9,10},{10,1... | collective-permute-start | bytes 491528 | tf_op jit(solution)/shard_map/ppermute | solution.py:85
  82.4 2.3 %collective-permute-start.1 = (bf16[2,64,640]{2,1,0:T(8,128)(2,1)S(1)}, bf16[2,64,640]{2,1,0:T(8,128)(2,1)S(1)}, u32[]{:S(2)}, u32[]{:S(2)}) collective-permute-start(bf16[2,64,640]{2,1,0:T(8,128)(2,1)S(1)} %pad_maximum_fusion.4), channel_id=1, source_target_pairs={{0,3},{1,0},{2,1},{3,2},{4,7},{5,4},{6,5},{7,6},{8,11},{9,8},{10,9... | collective-permute-start | bytes 491528 | tf_op jit(solution)/shard_map/ppermute | solution.py:87
  86.8 2.1 %fusion.14 = f32[2,64,640]{2,1,0:T(8,128)S(1)} fusion(bf16[2,640,2560]{2,1,0:T(8,128)(2,1)} %param.10, s32[]{:T(128)S(6)} %select_n.75, bf16[1,64,640]{2,1,0:T(8,128)(2,1)S(1)} %fusion.28, bf16[1,64,640]{2,1,0:T(8,128)(2,1)S(1)} %fusion.29), kind=kOutput, calls=%fused_computation.16 | convolution fusion | flops 104939520 | bytes 2129924 | tf_op jit(solution)/shard_map/icb,irb->icr/dot_general | solution.py:78
  89.8 2.1 %fusion.10 = f32[2,64,640]{2,1,0:T(8,128)S(1)} fusion(bf16[2,64,640]{2,1,0:T(8,128)(2,1)S(1)} %collective-permute-done.2, bf16[2,640,2560]{2,1,0:T(8,128)(2,1)} %param.10, s32[]{:T(128)S(6)} %select_n.79), kind=kOutput, calls=%fused_computation.12 | convolution fusion | flops 104857600 | bytes 2129924 | tf_op jit(solution)/shard_map/icb,irb->icr/dot_general | solution.py:96
  92.3 2.1 %fusion.19 = f32[2,64,640]{2,1,0:T(8,128)S(1)} fusion(f32[2,64,640]{2,1,0:T(8,128)S(1)} %fusion.10, f32[2,64,640]{2,1,0:T(8,128)S(1)} %fusion.14, bf16[2,64,640]{2,1,0:T(8,128)(2,1)S(1)} %collective-permute-done.1, bf16[2,640,2560]{2,1,0:T(8,128)(2,1)} %param.10, s32[]{:T(128)S(6)} %select_n.77), kind=kOutput, calls=%fused_computation.19 | convolution fusion | flops 105021440 | bytes 2785284 | tf_op jit(solution)/shard_map/icb,irb->icr/dot_general | solution.py:88
  94.4 2.6 %collective-permute-done.3 = bf16[2,64,640]{2,1,0:T(8,128)(2,1)S(1)} collective-permute-done((bf16[2,64,640]{2,1,0:T(8,128)(2,1)S(1)}, bf16[2,64,640]{2,1,0:T(8,128)(2,1)S(1)}, u32[]{:S(2)}, u32[]{:S(2)}) %collective-permute-start.3) | collective-permute-done | bytes 163872 | tf_op jit(solution)/shard_map/ppermute | solution.py:85
  97.0 2.1 %fusion.22 = f32[2,64,640]{2,1,0:T(8,128)S(1)} fusion(f32[2,64,640]{2,1,0:T(8,128)S(1)} %fusion.19, bf16[2,64,640]{2,1,0:T(8,128)(2,1)S(1)} %collective-permute-done.3, bf16[2,640,2560]{2,1,0:T(8,128)(2,1)} %param.10, s32[]{:T(128)S(6)} %select_n.81), kind=kOutput, calls=%fused_computation.20 | convolution fusion | flops 104939520 | bytes 2457604 | tf_op jit(solution)/shard_map/icb,irb->icr/dot_general | solution.py:96
  100.0 9.9 %all-gather.2 = f32[1024,128]{1,0:T(8,128)S(1)} all-gather(f32[128,128]{1,0:T(8,128)S(1)} %convolution_select_fusion), channel_id=4, replica_groups=mesh['chain'=8,'col'=4] {'chain'}, dimensions={0}, use_global_device_ids=true | all-gather | bytes 589824 | tf_op jit(solution)/shard_map/all_gather | solution.py:17
  109.9 23.5 %all-reduce.4.cloned.1.call-done = f32[2,64,128]{2,1,0:T(8,128)} async-done(((f32[2,64,128]{2,1,0:T(8,128)}), f32[2,64,128]{2,1,0:T(8,128)}) %all-reduce.4.cloned.1.call-update) | async-done | bytes 65552 | tf_op jit(solution)/shard_map/psum | solution.py:111
  135.3 9.3 %all-gather.3 = f32[512,128]{1,0:T(8,128)S(1)} all-gather(f32[64,128]{1,0:T(8,128)S(1)} %convolution_add_fusion.1), channel_id=5, replica_groups=mesh['chain'=8,'col'=4] {'chain'}, dimensions={0}, use_global_device_ids=true | all-gather | bytes 294912 | tf_op jit(solution)/shard_map/all_gather | solution.py:17
  144.5 1.6 %while.27 = (s32[]{:T(128)}, f32[64,128]{1,0:T(8,128)S(1)}, s32[]{:T(128)}, f32[8,128,128]{2,1,0:T(8,128)S(1)}, f32[8,64,128]{2,1,0:T(8,128)S(1)}, /*index=5*/s32[]{:T(128)}, s32[]{:T(128)}, s32[]{:T(128)}, s32[]{:T(128)}) while((s32[]{:T(128)}, f32[64,128]{1,0:T(8,128)S(1)}, s32[]{:T(128)}, f32[8,128,128]{2,1,0:T(8,128)S(1)}, ...), condition=%wide.region_7.8_spmd, body=%wide.region_6.7_spmd.sunk | while | flops 12591110 | bytes 230539 | solution.py:26
  (51 shorter events, 13.2 us)
Async XLA Ops:
  6.5 8.3 %copy-start = (bf16[64,640]{1,0:T(8,128)(2,1)S(1)}, bf16[64,640]{1,0:T(8,128)(2,1)}, u32[]{:S(2)}) copy-start(bf16[64,640]{1,0:T(8,128)(2,1)} %param.13) | copy-start | bytes 245764
  6.5 72.5 %copy-start.4 = (bf16[2,64,640]{2,1,0:T(8,128)(2,1)S(1)}, bf16[2,64,640]{2,1,0:T(8,128)(2,1)}, u32[]{:S(2)}) copy-start(bf16[2,64,640]{2,1,0:T(8,128)(2,1)} %param.9) | copy-start | bytes 491524
  6.5 72.5 %copy-start.2 = (bf16[2,640,128]{2,1,0:T(8,128)(2,1)S(1)}, bf16[2,640,128]{2,1,0:T(8,128)(2,1)}, u32[]{:S(2)}) copy-start(bf16[2,640,128]{2,1,0:T(8,128)(2,1)} %param.11) | copy-start | bytes 983044
  6.5 48.9 %all-reduce.6.cloned.1.call-start = ((), (), s32[]{:S(2)}) async-start(), calls=%async_computation.1 | async-start | bytes 393216 | tf_op jit(solution)/shard_map/psum | solution.py:51
  7.8 3.3 %collective-permute-start = (bf16[1,640,128]{1,2,0:T(8,128)(2,1)S(1)}, bf16[1,640,128]{1,2,0:T(8,128)(2,1)S(1)}, u32[]{:S(2)}, u32[]{:S(2)}) collective-permute-start(bf16[1,640,128]{1,2,0:T(8,128)(2,1)S(1)} %copy.10), channel_id=1, source_target_pairs={{4,0},{8,4},{12,8},{16,12},{20,16},{24,20},{28,24},{5,1},{9,5},{13... | collective-permute-start | bytes 491528 | tf_op jit(solution)/shard_map/ppermute | solution.py:10
  14.8 118.6 %all-reduce.4.cloned.1.call-start = ((), (), s32[]{:S(2)}) async-start(), calls=%async_computation | async-start | bytes 131072 | tf_op jit(solution)/shard_map/psum | solution.py:111
  79.0 54.4 %copy-start.1 = (f32[2,128,128]{1,2,0:T(8,128)S(1)}, f32[2,128,128]{1,2,0:T(8,128)}, u32[]{:S(2)}) copy-start(f32[2,128,128]{1,2,0:T(8,128)} %get-tuple-element.155) | copy-start | bytes 393220
  80.8 9.0 %collective-permute-start.2 = (bf16[2,64,640]{2,1,0:T(8,128)(2,1)S(1)}, bf16[2,64,640]{2,1,0:T(8,128)(2,1)S(1)}, u32[]{:S(2)}, u32[]{:S(2)}) collective-permute-start(bf16[2,64,640]{2,1,0:T(8,128)(2,1)S(1)} %pad_maximum_fusion.4), channel_id=1, source_target_pairs={{0,1},{1,2},{2,3},{3,0},{4,5},{5,6},{6,7},{7,4},{8,9},{9,10},{10,1... | collective-permute-start | bytes 491528 | tf_op jit(solution)/shard_map/ppermute | solution.py:85
  82.4 9.9 %collective-permute-start.1 = (bf16[2,64,640]{2,1,0:T(8,128)(2,1)S(1)}, bf16[2,64,640]{2,1,0:T(8,128)(2,1)S(1)}, u32[]{:S(2)}, u32[]{:S(2)}) collective-permute-start(bf16[2,64,640]{2,1,0:T(8,128)(2,1)S(1)} %pad_maximum_fusion.4), channel_id=1, source_target_pairs={{0,3},{1,0},{2,1},{3,2},{4,7},{5,4},{6,5},{7,6},{8,11},{9,8},{10,9... | collective-permute-start | bytes 491528 | tf_op jit(solution)/shard_map/ppermute | solution.py:87
  86.7 60.4 %copy-start.3 = (bf16[2,640,128]{2,1,0:T(8,128)(2,1)S(1)}, bf16[2,640,128]{2,1,0:T(8,128)(2,1)}, u32[]{:S(2)}) copy-start(bf16[2,640,128]{2,1,0:T(8,128)(2,1)} %param.12) | copy-start | bytes 983044
  89.8 7.3 %collective-permute-start.3 = (bf16[2,64,640]{2,1,0:T(8,128)(2,1)S(1)}, bf16[2,64,640]{2,1,0:T(8,128)(2,1)S(1)}, u32[]{:S(2)}, u32[]{:S(2)}) collective-permute-start(bf16[2,64,640]{2,1,0:T(8,128)(2,1)S(1)} %collective-permute-done.2), channel_id=1, source_target_pairs={{0,1},{1,2},{2,3},{3,0},{4,5},{5,6},{6,7},{7,4},{8,9},{9,10},{10,1... | collective-permute-start | bytes 491528 | tf_op jit(solution)/shard_map/ppermute | solution.py:85
Sparse Core Ops, SparseCore 0:
  14.9 40.4 all-reduce.5
  100.1 33.2 all-reduce.3
